TPU v7x, 128 devices: a whole 4x4x4 slice. The times are simulated.
128 devices in a mesh: comp: 16 (over y, z_hi, core), gx: 2 (over z_lo), gy: 4 (over x).
Axes of the slice: x: 4, y: 4, z: 4 (z_hi: 2, z_lo: 2; z = z_hi * 2 + z_lo), core: 2. Of those that a mesh axis runs over, the one named last changes fastest.
Arguments:
- field: float32 [16, 256, 64, 256], P('comp', 'gx', 'gy'), may hold values from -6 to 6
- third_level: int32 [16], replicated, may hold values from 2 to 6
- coefficients: int32 [16], replicated, may hold values from -3 to 3, as said below
- rates: float32 [2, 4], replicated, may hold values from 0.01 to 0.4, as said below
- reaction: float32 [1], replicated, may hold values from 0.1 to 0.3
Outputs:
- result: float32 [16, 256, 64, 256], P('comp', 'gx', 'gy')
Inputs may be any that keep to these rules, and one draw needn't show every extreme that they name: The fourth dimension of grid g has level 8 minus third_level[g]. `coefficients`: every weight is a nonzero integer; some are positive and some negative. `rates`: courant numbers of the first two dimensions lie from 0.3 to 0.4, all other entries from 0.01 to 0.02.
All inputs are finite; a program needn't handle non-finite values.
Results may differ from a plain program's by a relative error of at most 0.0003.
Values sent between devices are 32-bit elements; how exact they have to be, the bound alone decides.
A program may use at most 128 MiB of HBM per device.

v0:
```python
import functools

import jax
import jax.numpy as jnp
import ml_dtypes
import numpy as np
from jax import lax
from jax.experimental import pallas as pl
from jax.experimental.pallas import tpu as pltpu
from jax.sharding import PartitionSpec as P

MESH = pl.DeviceIdType.MESH
SECTIONS = 4
LEVEL_SUM = 8
LEVELS = (2, 3, 4, 5, 6)
FLAT = 256
GRIDS = 16
CHUNKS = 4
ORDER = [(1, 0), (0, 1), (3, 0), (1, 1), (2, 0), (3, 1), (2, 1)]
PEERS = [(y, z, c) for y, z in ORDER for c in (0, 1)] + [(0, 0, 1)]


def hat_matrix(fine, coarse):
    step = 2 ** (fine - coarse)
    count = 2**coarse
    out = np.zeros((2**fine, count), np.float64)
    for i in range(2**fine):
        left, part = divmod(i, step)
        out[i, left] += 1 - part / step
        out[i, (left + 1) % count] += part / step
    return out


def pick_matrix(coarse, fine):
    out = np.zeros((2**coarse, 2**fine), np.float64)
    out[np.arange(2**coarse), np.arange(2**coarse) * 2 ** (fine - coarse)] = 1
    return out


def between(low, high):
    return pick_matrix(low, high) if low <= high else hat_matrix(low, high)


def exchange_matrix(to, source):
    third = between(to, source)
    fourth = between(LEVEL_SUM - to, LEVEL_SUM - source)
    return np.kron(third, fourth).T


def exchange_table():
    out = np.stack(
        [
            np.concatenate([exchange_matrix(to, source) for source in LEVELS if source != to])
            for to in LEVELS
        ]
    )
    return out.astype(ml_dtypes.bfloat16)


def split(values):
    high = values.astype(jnp.bfloat16)
    return high, (values - high.astype(jnp.float32)).astype(jnp.bfloat16)


def dot(a, b):
    return jnp.dot(a, b, preferred_element_type=jnp.float32)


def kernel(
    field, table, level_ref, coef_ref, rate_ref, react_ref,
    out,
    u0, up8, dn8, ta, tb, mm, a_hi, a_lo, sent, got, lvl, res, back, tab,
    load_sem, tab_sem, hs_sem, hr_sem, s1, r1, s2, r2,
):
    rows = field.shape[0]
    cy = field.shape[1]
    per = rows // CHUNKS
    own = per // GRIDS
    comp, gx, gy = (lax.axis_index(a) for a in ("comp", "gx", "gy"))
    y, z, c = comp // 4, (comp // 2) % 2, comp % 2

    def mate(p, sign=1):
        return ((y + sign * p[0]) % 4) * 4 + ((z + p[1]) % 2) * 2 + (c + p[2]) % 2

    loads = [
        pltpu.make_async_copy(
            field.at[pl.ds(k * per, per)],
            u0.at[pl.ds(4 + k * per, per), pl.ds(0, cy)],
            load_sem.at[k],
        )
        for k in range(CHUNKS)
    ]
    for copy in loads:
        copy.start()
    tab_copy = pltpu.make_async_copy(table, tab, tab_sem)
    tab_copy.start()

    gxo = (gx + 1) % 2
    gyu, gyd = (gy + 1) % 4, (gy + 3) % 4
    near = [
        {"gx": gxo},
        {"gy": gyu},
        {"gy": gyd},
        {"gx": gxo, "gy": gyu},
        {"gx": gxo, "gy": gyd},
    ]
    barrier = pltpu.get_barrier_semaphore()
    for device in near + [{"comp": mate(p)} for p in PEERS]:
        pl.semaphore_signal(barrier, inc=1, device_id=device, device_id_type=MESH)

    level = level_ref[comp]
    coarse3 = jnp.float32(1.0)
    coarse4 = jnp.float32(1.0)
    for a in LEVELS:
        coarse3 = jnp.where(level == a, jnp.float32(2.0 ** (a - 6)), coarse3)
        coarse4 = jnp.where(level == a, jnp.float32(2.0 ** (2 - a)), coarse4)
    d0, d1 = rate_ref[0, 0], rate_ref[0, 1]
    d2, d3 = rate_ref[0, 2] * (coarse3 * coarse3), rate_ref[0, 3] * (coarse4 * coarse4)
    q0, q1 = rate_ref[1, 0], rate_ref[1, 1]
    q2, q3 = rate_ref[1, 2] * coarse3, rate_ref[1, 3] * coarse4
    rate = react_ref[0]
    keep = 1.0 - 2.0 * (d0 + d1 + d2 + d3) - (q0 + q1 + q2 + q3)
    width = jnp.int32(1)
    for a in LEVELS:
        width = jnp.where(level == a, jnp.int32(2 ** (LEVEL_SUM - a)), width)

    def neighbours(t, carry):
        at = t * 8 + lax.broadcasted_iota(jnp.int32, (8, FLAT), 0)
        to = lax.broadcasted_iota(jnp.int32, (8, FLAT), 1)
        inner = jnp.bitwise_and(to, width - 1)
        base = to - inner
        value = jnp.where(at == jnp.bitwise_and(to + width, FLAT - 1), d2, 0.0)
        value += jnp.where(at == jnp.bitwise_and(to - width, FLAT - 1), d2 + q2, 0.0)
        value += jnp.where(at == base + jnp.bitwise_and(inner + 1, width - 1), d3, 0.0)
        value += jnp.where(at == base + jnp.bitwise_and(inner - 1, width - 1), d3 + q3, 0.0)
        mm[pl.ds(t * 8, 8)] = value
        return carry

    lax.fori_loop(0, FLAT // 8, neighbours, 0)
    high, low = split(mm[pl.ds(0, FLAT)])
    a_hi[...] = high
    a_lo[...] = low

    for copy in loads:
        copy.wait()
    pl.semaphore_wait(barrier, len(near) + len(PEERS))

    def send(i, src, dst, device):
        copy = pltpu.make_async_remote_copy(
            src, dst, hs_sem.at[i], hr_sem.at[i], device_id=device, device_id_type=MESH
        )
        copy.start()
        return copy

    lo_tile, hi_tile = pl.ds(0, 8), pl.ds(cy - 8, 8)
    first, last = pl.ds(4, 4), pl.ds(rows, 4)
    before, after = pl.ds(0, 4), pl.ds(rows + 4, 4)
    body = pl.ds(0, cy)
    head = [
        send(0, u0.at[last, body], u0.at[before, body], {"gx": gxo}),
        send(1, u0.at[last, lo_tile], up8.at[before], {"gx": gxo, "gy": gyd}),
        send(2, u0.at[last, hi_tile], dn8.at[before], {"gx": gxo, "gy": gyu}),
    ]
    tail = [
        send(3, u0.at[first, body], u0.at[after, body], {"gx": gxo}),
        send(4, u0.at[first, lo_tile], up8.at[after], {"gx": gxo, "gy": gyd}),
        send(5, u0.at[first, hi_tile], dn8.at[after], {"gx": gxo, "gy": gyu}),
    ]
    sides = []
    for k in range(CHUNKS):
        begin = 4 if k == 0 else 8 + k * per
        end = rows + 4 if k == CHUNKS - 1 else 8 + (k + 1) * per
        part = pl.ds(begin, end - begin)
        sides.append(
            [
                send(6 + 2 * k, u0.at[part, lo_tile], up8.at[part], {"gy": gyd}),
                send(7 + 2 * k, u0.at[part, hi_tile], dn8.at[part], {"gy": gyu}),
            ]
        )

    def section(src, src_first, dst, count, final):
        def block(b, carry):
            r0 = src_first + b * 8
            flat = src[pl.ds(r0, 8)].reshape(8 * 24, FLAT)
            high, low = split(flat)
            mm[pl.ds(0, 192)] = dot(high, a_hi[...]) + dot(low, a_hi[...]) + dot(high, a_lo[...])
            for i in range(8):
                centre = src[r0 + i]
                above, below = src[r0 + i + 1], src[r0 + i - 1]
                value = (keep + rate / (1.0 + centre * centre)) * centre
                value += d0 * above + (d0 + q0) * below
                value += d1 * pltpu.roll(centre, 23, 0) + (d1 + q1) * pltpu.roll(centre, 1, 0)
                value += mm[pl.ds(i * 24, 24)]
                if final is None:
                    dst[b * 8 + i] = value
                else:
                    dst[final + b * 8 + i] = value[:cy]
            return carry

        lax.fori_loop(0, count // 8, block, 0)

    def forward(k):
        def copy(i, p, device):
            return pltpu.make_async_remote_copy(
                sent.at[pl.ds(k * per + device * own, own)],
                got.at[k, comp],
                s1.at[k, i],
                r1.at[k, i],
                device_id={"comp": device},
                device_id_type=MESH,
            )

        return [copy(i, p, mate(p)) for i, p in enumerate(PEERS)]

    def backward(k):
        def copy(i, p, device):
            return pltpu.make_async_remote_copy(
                back.at[k, device],
                out.at[pl.ds(k * per + comp * own, own)],
                s2.at[k, i],
                r2.at[k, i],
                device_id={"comp": device},
                device_id_type=MESH,
            )

        return [copy(i, p, mate(p)) for i, p in enumerate(PEERS)]

    lane_low = lax.broadcasted_iota(jnp.int32, (8, FLAT), 0) < 4

    def stencil(k):
        def halo(t, carry):
            r = k * per + t
            u0[r, pl.ds(cy, 8)] = jnp.where(lane_low, up8[r], dn8[r])
            return carry

        lax.fori_loop(0, per + 8, halo, 0)
        section(u0, k * per + 1, ta, per + 6 + 2, None)
        section(ta, 1, tb, per + 4 + 4, None)
        section(tb, 1, ta, per + 2 + 6, None)
        section(ta, 1, sent, per, k * per)

    flat_rows = own * cy

    def place(a):
        return jnp.clip(a - LEVELS[0], 0, len(LEVELS) - 1)

    def combine(k):
        for copy in forward(k):
            copy.wait_recv()
        got[k, comp] = sent[pl.ds(k * per + comp * own, own)]
        for n, a in enumerate(LEVELS):
            total = jnp.zeros((own, cy, FLAT), jnp.float32)
            for g in range(GRIDS):
                weight = jnp.where(level_ref[g] == a, coef_ref[g], 0).astype(jnp.float32)
                total += weight * got[k, g]
            total = total.reshape(flat_rows, FLAT)
            res[n] = total
            high, low = split(total)
            lvl[n, pl.ds(0, flat_rows)] = high
            lvl[n, pl.ds(flat_rows, flat_rows)] = low
        for n, a in enumerate(LEVELS):
            value = jnp.zeros((2 * flat_rows, FLAT), jnp.float32)
            for m, other in enumerate([o for o in range(len(LEVELS)) if o != n]):
                value += dot(lvl[other], tab[n, pl.ds(m * FLAT, FLAT)])
            res[n] += value[:flat_rows] + value[flat_rows:]
        for g in range(GRIDS):
            back[k, g] = res[place(level_ref[g])].reshape(own, cy, FLAT)
        out[pl.ds(k * per + comp * own, own)] = res[place(level)].reshape(own, cy, FLAT)
        for copy in backward(k):
            copy.start()

    for k in range(CHUNKS):
        for copy in sides[k]:
            copy.wait_recv()
        if k == 0:
            for copy in head:
                copy.wait_recv()
        if k == CHUNKS - 1:
            for copy in tail:
                copy.wait_recv()
        stencil(k)
        for copy in forward(k):
            copy.start()
        if k == 0:
            tab_copy.wait()
        else:
            combine(k - 1)
    combine(CHUNKS - 1)
    for copy in head + tail + sum(sides, []):
        copy.wait_send()
    for k in range(CHUNKS):
        for copy in forward(k):
            copy.wait_send()
        for copy in backward(k):
            copy.wait()


def solution(mesh):
    table = exchange_table()

    def local(field, third_level, coefficients, rates, reaction):
        _, rows, cy, flat = field.shape
        per = rows // CHUNKS
        own = per // GRIDS
        vmem, smem, anys = (
            pl.BlockSpec(memory_space=m) for m in (pltpu.VMEM, pltpu.SMEM, pl.ANY)
        )
        f32, bf16 = jnp.float32, jnp.bfloat16
        dma = pltpu.SemaphoreType.DMA
        peers = len(PEERS)
        halos = 6 + 2 * CHUNKS
        result = pl.pallas_call(
            kernel,
            out_shape=jax.ShapeDtypeStruct((rows, cy, flat), f32),
            in_specs=[anys, anys, smem, smem, smem, smem],
            out_specs=vmem,
            scratch_shapes=[
                pltpu.VMEM((rows + 8 + 8, cy + 8, flat), f32),
                pltpu.VMEM((rows + 8, 8, flat), f32),
                pltpu.VMEM((rows + 8, 8, flat), f32),
                pltpu.VMEM((per + 16, cy + 8, flat), f32),
                pltpu.VMEM((per + 16, cy + 8, flat), f32),
                pltpu.VMEM((max(8 * (cy + 8), flat), flat), f32),
                pltpu.VMEM((flat, flat), bf16),
                pltpu.VMEM((flat, flat), bf16),
                pltpu.VMEM((rows, cy, flat), f32),
                pltpu.VMEM((CHUNKS, GRIDS, own, cy, flat), f32),
                pltpu.VMEM((len(LEVELS), 2 * own * cy, flat), bf16),
                pltpu.VMEM((len(LEVELS), own * cy, flat), f32),
                pltpu.VMEM((CHUNKS, GRIDS, own, cy, flat), f32),
                pltpu.VMEM(table.shape, bf16),
                dma((CHUNKS,)),
                dma,
                dma((halos,)),
                dma((halos,)),
                dma((CHUNKS, peers)),
                dma((CHUNKS, peers)),
                dma((CHUNKS, peers)),
                dma((CHUNKS, peers)),
            ],
            compiler_params=pltpu.CompilerParams(
                collective_id=0, has_side_effects=True, vmem_limit_bytes=40 << 20
            ),
        )(field[0], jnp.asarray(table), third_level, coefficients, rates, reaction)
        return result[None]

    return jax.shard_map(
        local,
        mesh=mesh,
        in_specs=(P("comp", "gx", "gy", None), P(), P(), P(), P()),
        out_specs=P("comp", "gx", "gy", None),
        check_vma=False,
    )
```

profile of v0, /device:TPU:1, one launch (start us, length us, event | category | flops | bytes accessed | tf_op | source)
XLA Modules:
  0.0 84.3 jit_solution(5157814975337284476)
XLA Ops:
  0.7 0.0 copy-start
  0.7 1.7 %copy-done = bf16[5,1024,256]{2,1,0:T(8,128)(2,1)S(1)} copy-done((bf16[5,1024,256]{2,1,0:T(8,128)(2,1)S(1)}, bf16[5,1024,256]{2,1,0:T(8,128)(2,1)}, u32[]{:S(2)}) %copy-start) | copy-done | bytes 2621464
  2.4 0.0 copy-start.1
  2.4 1.6 %copy-done.1 = f32[1,128,16,256]{3,2,1,0:T(8,128)S(1)} copy-done((f32[1,128,16,256]{3,2,1,0:T(8,128)S(1)}, f32[1,128,16,256]{3,2,1,0:T(8,128)}, u32[]{:S(2)}) %copy-start.1) | copy-done | bytes 2097176
  4.0 0.0 copy-start.2
  4.0 0.7 copy-done.2
  4.7 0.0 copy-start.3
  4.7 0.7 copy-done.3
  5.3 0.0 copy-start.4
  5.3 0.7 copy-done.4
  6.0 77.0 %shard_map.64 = f32[128,16,256]{2,1,0:T(8,128)S(1)} custom-call(f32[128,16,256]{2,1,0:T(8,128)S(1)} %bitcast.3, bf16[5,1024,256]{2,1,0:T(8,128)(2,1)S(1)} %copy-done, s32[16]{0:T(128)S(1)} %copy-done.3, s32[16]{0:T(128)S(1)} %copy-done.4, f32[2,4]{1,0:T(2,128)S(1)} %copy-done.2, f32[1]{0:T(128)S(6)} %copy.8.react_ref), custom_call_target="tpu_custom_call" | custom-call | tf_op jit(solution)/shard_map/pallas_call | solution.py:312
  83.0 1.3 %copy.9 = f32[1,128,16,256]{3,2,1,0:T(8,128)} copy(f32[1,128,16,256]{3,2,1,0:T(8,128)S(1)} %bitcast.2) | data formatting | bytes 4194304
Async XLA Ops:
  0.7 1.7 %copy-start = (bf16[5,1024,256]{2,1,0:T(8,128)(2,1)S(1)}, bf16[5,1024,256]{2,1,0:T(8,128)(2,1)}, u32[]{:S(2)}) copy-start(bf16[5,1024,256]{2,1,0:T(8,128)(2,1)} %constant.2.clone.table) | copy-start | bytes 7864324
  2.4 1.6 %copy-start.1 = (f32[1,128,16,256]{3,2,1,0:T(8,128)S(1)}, f32[1,128,16,256]{3,2,1,0:T(8,128)}, u32[]{:S(2)}) copy-start(f32[1,128,16,256]{3,2,1,0:T(8,128)} %param.6) | copy-start | bytes 6291460
  4.0 0.7 copy-start.2
  4.7 0.7 copy-start.3
  5.3 0.7 copy-start.4
where the time goes:
time: 84.5 us; the launch traced here: 84.3 us
  Pallas kernels  77 us (91%)
  local copies, waits for them, and re-layouts  6.64 us (8%)
    pallas_call x1, Pallas kernels, local(): pl.pallas_call(kernel, out_shape=jax.ShapeDtypeStruct((rows, cy, flat), f...  77 us
    unnamed x11, local copies, waits for them, and re-layouts  6.64 us

commit v1 on v0

--- a/solution.py
+++ b/solution.py
@@ -67,9 +67,10 @@
 
 
 def kernel(
-    field, table, level_ref, coef_ref, rate_ref, react_ref,
+    field, table, level_in, coef_in, rate_in, react_in,
     out,
-    u0, up8, dn8, ta, tb, mm, a_hi, a_lo, sent, got, lvl, res, back, tab,
+    level_ref, coef_ref, rate_ref, react_ref, small_sem,
+    u0, pack_up, pack_dn, up8, dn8, ta, tb, mm, a_hi, a_lo, sent, got, lvl, res, back, tab,
     load_sem, tab_sem, hs_sem, hr_sem, s1, r1, s2, r2,
 ):
     rows = field.shape[0]
@@ -90,7 +91,13 @@
         )
         for k in range(CHUNKS)
     ]
-    for copy in loads:
+    smalls = [
+        pltpu.make_async_copy(src, dst, small_sem.at[i])
+        for i, (src, dst) in enumerate(
+            [(level_in, level_ref), (rate_in, rate_ref), (react_in, react_ref), (coef_in, coef_ref)]
+        )
+    ]
+    for copy in smalls + loads:
         copy.start()
     tab_copy = pltpu.make_async_copy(table, tab, tab_sem)
     tab_copy.start()
@@ -108,6 +115,8 @@
     for device in near + [{"comp": mate(p)} for p in PEERS]:
         pl.semaphore_signal(barrier, inc=1, device_id=device, device_id_type=MESH)
 
+    for copy in smalls:
+        copy.wait()
     level = level_ref[comp]
     coarse3 = jnp.float32(1.0)
     coarse4 = jnp.float32(1.0)
@@ -143,6 +152,27 @@
 
     for copy in loads:
         copy.wait()
+
+    lane_low = lax.broadcasted_iota(jnp.int32, (8, FLAT), 0) < 4
+    lo_tile, hi_tile = pl.ds(0, 8), pl.ds(cy - 8, 8)
+
+    def pack(begin, end):
+        def pair(m, carry):
+            even, odd = u0[2 * m, lo_tile], u0[2 * m + 1, lo_tile]
+            pack_up[m] = jnp.where(lane_low, even, pltpu.roll(odd, 4, 0))
+            even, odd = u0[2 * m, hi_tile], u0[2 * m + 1, hi_tile]
+            pack_dn[m] = jnp.where(lane_low, pltpu.roll(odd, 4, 0), even)
+            return carry
+
+        lax.fori_loop(begin // 2, end // 2, pair, 0)
+
+    parts = []
+    for k in range(CHUNKS):
+        begin = 4 if k == 0 else 8 + k * per
+        end = rows + 4 if k == CHUNKS - 1 else 8 + (k + 1) * per
+        parts.append((begin, end))
+    pack(*parts[0])
+    pack(rows, rows + 4)
     pl.semaphore_wait(barrier, len(near) + len(PEERS))
 
     def send(i, src, dst, device):
@@ -152,31 +182,37 @@
         copy.start()
         return copy
 
-    lo_tile, hi_tile = pl.ds(0, 8), pl.ds(cy - 8, 8)
-    first, last = pl.ds(4, 4), pl.ds(rows, 4)
-    before, after = pl.ds(0, 4), pl.ds(rows + 4, 4)
+    def half(begin, end):
+        return pl.ds(begin // 2, (end - begin) // 2)
+
     body = pl.ds(0, cy)
-    head = [
-        send(0, u0.at[last, body], u0.at[before, body], {"gx": gxo}),
-        send(1, u0.at[last, lo_tile], up8.at[before], {"gx": gxo, "gy": gyd}),
-        send(2, u0.at[last, hi_tile], dn8.at[before], {"gx": gxo, "gy": gyu}),
-    ]
-    tail = [
-        send(3, u0.at[first, body], u0.at[after, body], {"gx": gxo}),
-        send(4, u0.at[first, lo_tile], up8.at[after], {"gx": gxo, "gy": gyd}),
-        send(5, u0.at[first, hi_tile], dn8.at[after], {"gx": gxo, "gy": gyu}),
-    ]
     sides = []
-    for k in range(CHUNKS):
-        begin = 4 if k == 0 else 8 + k * per
-        end = rows + 4 if k == CHUNKS - 1 else 8 + (k + 1) * per
-        part = pl.ds(begin, end - begin)
+
+    def send_side(k):
+        part = half(*parts[k])
         sides.append(
             [
-                send(6 + 2 * k, u0.at[part, lo_tile], up8.at[part], {"gy": gyd}),
-                send(7 + 2 * k, u0.at[part, hi_tile], dn8.at[part], {"gy": gyu}),
+                send(6 + 2 * k, pack_up.at[part], up8.at[part], {"gy": gyd}),
+                send(7 + 2 * k, pack_dn.at[part], dn8.at[part], {"gy": gyu}),
             ]
         )
+
+    lasts, before = half(rows, rows + 4), half(0, 4)
+    head = [
+        send(0, u0.at[pl.ds(rows, 4), body], u0.at[pl.ds(0, 4), body], {"gx": gxo}),
+        send(1, pack_up.at[lasts], up8.at[before], {"gx": gxo, "gy": gyd}),
+        send(2, pack_dn.at[lasts], dn8.at[before], {"gx": gxo, "gy": gyu}),
+    ]
+    send_side(0)
+    for k in range(1, CHUNKS):
+        pack(parts[k][0], min(parts[k][1], rows))
+        send_side(k)
+    firsts, after = half(4, 8), half(rows + 4, rows + 8)
+    tail = [
+        send(3, u0.at[pl.ds(4, 4), body], u0.at[pl.ds(rows + 4, 4), body], {"gx": gxo}),
+        send(4, pack_up.at[firsts], up8.at[after], {"gx": gxo, "gy": gyd}),
+        send(5, pack_dn.at[firsts], dn8.at[after], {"gx": gxo, "gy": gyu}),
+    ]
 
     def section(src, src_first, dst, count, final):
         def block(b, carry):
@@ -225,15 +261,15 @@
 
         return [copy(i, p, mate(p)) for i, p in enumerate(PEERS)]
 
-    lane_low = lax.broadcasted_iota(jnp.int32, (8, FLAT), 0) < 4
-
     def stencil(k):
         def halo(t, carry):
-            r = k * per + t
-            u0[r, pl.ds(cy, 8)] = jnp.where(lane_low, up8[r], dn8[r])
+            m = k * (per // 2) + t
+            up, dn = up8[m], dn8[m]
+            u0[2 * m, pl.ds(cy, 8)] = jnp.where(lane_low, up, dn)
+            u0[2 * m + 1, pl.ds(cy, 8)] = pltpu.roll(jnp.where(lane_low, dn, up), 4, 0)
             return carry
 
-        lax.fori_loop(0, per + 8, halo, 0)
+        lax.fori_loop(0, per // 2 + 4, halo, 0)
         section(u0, k * per + 1, ta, per + 6 + 2, None)
         section(ta, 1, tb, per + 4 + 4, None)
         section(tb, 1, ta, per + 2 + 6, None)
@@ -302,9 +338,7 @@
         _, rows, cy, flat = field.shape
         per = rows // CHUNKS
         own = per // GRIDS
-        vmem, smem, anys = (
-            pl.BlockSpec(memory_space=m) for m in (pltpu.VMEM, pltpu.SMEM, pl.ANY)
-        )
+        vmem, hbm = (pl.BlockSpec(memory_space=m) for m in (pltpu.VMEM, pltpu.HBM))
         f32, bf16 = jnp.float32, jnp.bfloat16
         dma = pltpu.SemaphoreType.DMA
         peers = len(PEERS)
@@ -312,12 +346,19 @@
         result = pl.pallas_call(
             kernel,
             out_shape=jax.ShapeDtypeStruct((rows, cy, flat), f32),
-            in_specs=[anys, anys, smem, smem, smem, smem],
+            in_specs=[hbm] * 6,
             out_specs=vmem,
             scratch_shapes=[
+                pltpu.SMEM(third_level.shape, jnp.int32),
+                pltpu.SMEM(coefficients.shape, jnp.int32),
+                pltpu.SMEM(rates.shape, f32),
+                pltpu.SMEM(reaction.shape, f32),
+                dma((4,)),
                 pltpu.VMEM((rows + 8 + 8, cy + 8, flat), f32),
-                pltpu.VMEM((rows + 8, 8, flat), f32),
-                pltpu.VMEM((rows + 8, 8, flat), f32),
+                pltpu.VMEM((rows // 2 + 4, 8, flat), f32),
+                pltpu.VMEM((rows // 2 + 4, 8, flat), f32),
+                pltpu.VMEM((rows // 2 + 4, 8, flat), f32),
+                pltpu.VMEM((rows // 2 + 4, 8, flat), f32),
                 pltpu.VMEM((per + 16, cy + 8, flat), f32),
                 pltpu.VMEM((per + 16, cy + 8, flat), f32),
                 pltpu.VMEM((max(8 * (cy + 8), flat), flat), f32),
@@ -339,7 +380,7 @@
                 dma((CHUNKS, peers)),
             ],
             compiler_params=pltpu.CompilerParams(
-                collective_id=0, has_side_effects=True, vmem_limit_bytes=40 << 20
+                collective_id=0, has_side_effects=True, vmem_limit_bytes=64900000
             ),
         )(field[0], jnp.asarray(table), third_level, coefficients, rates, reaction)
         return result[None]

time: 84.5 us -> 76.7 us (0.908)
  Pallas kernels: 77 us -> 72.9 us
  local copies, waits for them, and re-layouts: 6.64 us -> 3.08 us
    pallas_call x1, Pallas kernels: 77 us -> 72.9 us  [local(): pl.pallas_call(kernel, out_shape=jax.ShapeDtypeStruct((rows, cy, flat), f...]
    unnamed x11 -> x1, local copies, waits for them, and re-layouts: 6.64 us -> 3.08 us
where the time goes in v1:
time: 76.7 us; the launch traced here: 76.6 us
  Pallas kernels  72.9 us (95%)
  local copies, waits for them, and re-layouts  3.08 us (4%)
    pallas_call x1, Pallas kernels, local(): pl.pallas_call(kernel, out_shape=jax.ShapeDtypeStruct((rows, cy, flat), f...  72.9 us
    unnamed x1, local copies, waits for them, and re-layouts  3.08 us

profile of v1, /device:TPU:1, one launch (start us, length us, event | category | flops | bytes accessed | tf_op | source)
XLA Modules:
  0.0 76.6 jit_solution(5895119508945383961)
XLA Ops:
  0.7 72.9 %shard_map.64 = f32[128,16,256]{2,1,0:T(8,128)} custom-call(f32[128,16,256]{2,1,0:T(8,128)} %bitcast.3, bf16[5,1024,256]{2,1,0:T(8,128)(2,1)} %constant.2.clone.table, s32[16]{0:T(128)} %level_in.1, s32[16]{0:T(128)} %coef_in.1, f32[2,4]{1,0:T(2,128)} %rate_in.1, f32[1]{0:T(128)S(6)} %copy.8.react_in), custom_call_target="tpu_custom_call" | custom-call | tf_op jit(solution)/shard_map/pallas_call | solution.py:346
  73.5 3.1 %copy.9 = f32[1,128,16,256]{3,2,1,0:T(8,128)} copy(f32[1,128,16,256]{3,2,1,0:T(8,128)} %bitcast.2) | data formatting | bytes 4194304

commit v2 on v1

v2 whole, which is shorter than its diff:
```python
import functools

import jax
import jax.numpy as jnp
import ml_dtypes
import numpy as np
from jax import lax
from jax.experimental import pallas as pl
from jax.experimental.pallas import tpu as pltpu
from jax.sharding import PartitionSpec as P

MESH = pl.DeviceIdType.MESH
SECTIONS = 4
LEVEL_SUM = 8
LEVELS = (2, 3, 4, 5, 6)
FLAT = 256
GRIDS = 16
BLOCK = 16
ORDER = [(1, 0), (0, 1), (3, 0), (1, 1), (2, 0), (3, 1), (2, 1)]
PEERS = [(y, z, c) for y, z in ORDER for c in (0, 1)] + [(0, 0, 1)]


def hat_matrix(fine, coarse):
    step = 2 ** (fine - coarse)
    count = 2**coarse
    out = np.zeros((2**fine, count), np.float64)
    for i in range(2**fine):
        left, part = divmod(i, step)
        out[i, left] += 1 - part / step
        out[i, (left + 1) % count] += part / step
    return out


def pick_matrix(coarse, fine):
    out = np.zeros((2**coarse, 2**fine), np.float64)
    out[np.arange(2**coarse), np.arange(2**coarse) * 2 ** (fine - coarse)] = 1
    return out


def between(low, high):
    return pick_matrix(low, high) if low <= high else hat_matrix(low, high)


def exchange_matrix(to, source):
    third = between(to, source)
    fourth = between(LEVEL_SUM - to, LEVEL_SUM - source)
    return np.kron(third, fourth).T


def exchange_table():
    out = np.stack(
        [
            np.concatenate([exchange_matrix(to, source) for source in LEVELS if source != to])
            for to in LEVELS
        ]
    )
    return out.astype(ml_dtypes.bfloat16)


def split(values):
    high = values.astype(jnp.bfloat16)
    return high, (values - high.astype(jnp.float32)).astype(jnp.bfloat16)


def dot(a, b):
    return jnp.dot(a, b, preferred_element_type=jnp.float32)


def kernel(
    field, table, level_in, coef_in, rate_in, react_in,
    land,
    level_ref, coef_ref, rate_ref, react_ref, small_sem,
    u0, pack_up, pack_dn, up8, dn8, ta, tb, mm, a_hi, a_lo, sent, got, lvl, res, back, mine, mine_sem, tab,
    load_sem, tab_sem, hs_sem, hr_sem, s1, r1, s2, r2,
):
    rows, cy = field.shape[0], field.shape[1]
    per = rows // 2
    own = per // GRIDS
    comp, gx, gy = (lax.axis_index(a) for a in ("comp", "gx", "gy"))
    y, z, c = comp // 4, (comp // 2) % 2, comp % 2

    def mate(p, sign=1):
        return ((y + sign * p[0]) % 4) * 4 + ((z + p[1]) % 2) * 2 + (c + p[2]) % 2

    quarter = rows // 4
    loads = [
        pltpu.make_async_copy(
            field.at[pl.ds(k * quarter, quarter)],
            u0.at[pl.ds(4 + k * quarter, quarter), pl.ds(0, cy)],
            load_sem.at[k],
        )
        for k in range(4)
    ]
    smalls = [
        pltpu.make_async_copy(src, dst, small_sem.at[i])
        for i, (src, dst) in enumerate(
            [(level_in, level_ref), (rate_in, rate_ref), (react_in, react_ref), (coef_in, coef_ref)]
        )
    ]
    for copy in smalls + loads:
        copy.start()
    tab_copy = pltpu.make_async_copy(table, tab, tab_sem)
    tab_copy.start()

    gxo = (gx + 1) % 2
    gyu, gyd = (gy + 1) % 4, (gy + 3) % 4
    near = [
        {"gx": gxo},
        {"gy": gyu},
        {"gy": gyd},
        {"gx": gxo, "gy": gyu},
        {"gx": gxo, "gy": gyd},
    ]
    barrier = pltpu.get_barrier_semaphore()
    for device in near + [{"comp": mate(p)} for p in PEERS]:
        pl.semaphore_signal(barrier, inc=1, device_id=device, device_id_type=MESH)

    for copy in smalls:
        copy.wait()
    level = level_ref[comp]
    coarse3 = jnp.float32(1.0)
    coarse4 = jnp.float32(1.0)
    for a in LEVELS:
        coarse3 = jnp.where(level == a, jnp.float32(2.0 ** (a - 6)), coarse3)
        coarse4 = jnp.where(level == a, jnp.float32(2.0 ** (2 - a)), coarse4)
    d0, d1 = rate_ref[0, 0], rate_ref[0, 1]
    d2, d3 = rate_ref[0, 2] * (coarse3 * coarse3), rate_ref[0, 3] * (coarse4 * coarse4)
    q0, q1 = rate_ref[1, 0], rate_ref[1, 1]
    q2, q3 = rate_ref[1, 2] * coarse3, rate_ref[1, 3] * coarse4
    rate = react_ref[0]
    keep = 1.0 - 2.0 * (d0 + d1 + d2 + d3) - (q0 + q1 + q2 + q3)
    width = jnp.int32(1)
    for a in LEVELS:
        width = jnp.where(level == a, jnp.int32(2 ** (LEVEL_SUM - a)), width)

    def neighbours(t, carry):
        at = t * 16 + lax.broadcasted_iota(jnp.int32, (16, FLAT), 0)
        to = lax.broadcasted_iota(jnp.int32, (16, FLAT), 1)
        inner = jnp.bitwise_and(to, width - 1)
        base = to - inner
        value = jnp.where(at == jnp.bitwise_and(to + width, FLAT - 1), d2, 0.0)
        value += jnp.where(at == jnp.bitwise_and(to - width, FLAT - 1), d2 + q2, 0.0)
        value += jnp.where(at == base + jnp.bitwise_and(inner + 1, width - 1), d3, 0.0)
        value += jnp.where(at == base + jnp.bitwise_and(inner - 1, width - 1), d3 + q3, 0.0)
        high, low = split(value)
        part = pl.ds(pl.multiple_of(t * 16, 16), 16)
        a_hi[part] = high
        a_lo[part] = low
        return carry

    lax.fori_loop(0, FLAT // 16, neighbours, 0)
    for copy in loads:
        copy.wait()

    def section(src, src_first, dst, dst_first, count, size, tall, final):
        kept = cy if final else tall
        flat = size * kept

        def block(b, carry):
            r0 = src_first + b * size
            high, low = split(src[pl.ds(r0, size), pl.ds(0, kept)].reshape(flat, FLAT))
            both = dot(jnp.concatenate([high, low]), a_hi[...])
            mm[pl.ds(0, flat)] = both[:flat] + both[flat:] + dot(high, a_lo[...])
            for i in range(size):
                whole = src[r0 + i, pl.ds(0, tall)]
                centre = whole[:kept]
                above, below = src[r0 + i + 1, pl.ds(0, kept)], src[r0 + i - 1, pl.ds(0, kept)]
                value = (keep + rate / (1.0 + centre * centre)) * centre
                value += d0 * above + (d0 + q0) * below
                value += d1 * pltpu.roll(whole, tall - 1, 0)[:kept]
                value += (d1 + q1) * pltpu.roll(whole, 1, 0)[:kept]
                value += mm[pl.ds(i * kept, kept)]
                if final == "inner":
                    low4, high4 = pltpu.roll(value[:8], 4, 0), pltpu.roll(value[8:16], 4, 0)
                    value = jnp.where(lane_low, low4, high4)
                elif final == "outer":
                    value = jnp.where(lane_low, value[:8], value[8:16])
                if final is None:
                    dst[dst_first + b * size + i, pl.ds(0, tall)] = value
                else:
                    dst[dst_first + b * size + i] = value
            return carry

        lax.fori_loop(0, count // size, block, 0)

    lane_low = lax.broadcasted_iota(jnp.int32, (8, FLAT), 0) < 4
    lo_tile, hi_tile = pl.ds(0, 8), pl.ds(cy - 8, 8)

    def early(first, count, tall):
        size = next(n for n in range(14, 32) if (count + 6) % n == 0)
        section(u0, first + 1, ta, 0, count + 6, size, tall, None)
        section(ta, 1, tb, 0, count + 6, size, tall, None)
        section(tb, 1, ta, 0, count + 6, size, tall, None)

    def late(count, tall, final, at):
        section(ta, 1, sent, at, count, BLOCK, tall, final)

    def pack(m, carry):
        even, odd = u0[2 * m, lo_tile], u0[2 * m + 1, lo_tile]
        pack_up[m] = jnp.where(lane_low, even, pltpu.roll(odd, 4, 0))
        even, odd = u0[2 * m, hi_tile], u0[2 * m + 1, hi_tile]
        pack_dn[m] = jnp.where(lane_low, pltpu.roll(odd, 4, 0), even)
        return carry

    lax.fori_loop(2, rows // 2 + 2, pack, 0)

    def send(i, src, dst, device):
        return pltpu.make_async_remote_copy(
            src, dst, hs_sem.at[i], hr_sem.at[i], device_id=device, device_id_type=MESH
        )

    def half(begin, end):
        return pl.ds(begin // 2, (end - begin) // 2)

    body = pl.ds(0, cy)
    lasts, before = half(rows, rows + 4), half(0, 4)
    firsts, after = half(4, 8), half(rows + 4, rows + 8)
    rims = [
        send(0, u0.at[pl.ds(rows, 4), body], u0.at[pl.ds(0, 4), body], {"gx": gxo}),
        send(3, u0.at[pl.ds(4, 4), body], u0.at[pl.ds(rows + 4, 4), body], {"gx": gxo}),
    ]
    corners = [
        send(1, pack_up.at[lasts], up8.at[before], {"gx": gxo, "gy": gyd}),
        send(2, pack_dn.at[lasts], dn8.at[before], {"gx": gxo, "gy": gyu}),
        send(4, pack_up.at[firsts], up8.at[after], {"gx": gxo, "gy": gyd}),
        send(5, pack_dn.at[firsts], dn8.at[after], {"gx": gxo, "gy": gyu}),
    ]
    sides = []
    for k, (begin, end) in enumerate([(4, per + 8), (per + 8, rows + 4)]):
        part = half(begin, end)
        sides.append(
            [
                send(6 + 2 * k, pack_up.at[part], up8.at[part], {"gy": gyd}),
                send(7 + 2 * k, pack_dn.at[part], dn8.at[part], {"gy": gyu}),
            ]
        )

    def forward(k):
        def copy(i, device):
            return pltpu.make_async_remote_copy(
                sent.at[pl.ds(k * per + device * own, own)],
                got.at[k, comp],
                s1.at[k, i],
                r1.at[k, i],
                device_id={"comp": device},
                device_id_type=MESH,
            )

        return [copy(i, mate(p)) for i, p in enumerate(PEERS)]

    def backward(k):
        def copy(i, device):
            return pltpu.make_async_remote_copy(
                back.at[k, device],
                land.at[pl.ds(k * per + comp * own, own)],
                s2.at[k, i],
                r2.at[k, i],
                device_id={"comp": device},
                device_id_type=MESH,
            )

        return [copy(i, mate(p)) for i, p in enumerate(PEERS)]

    flat_rows = own * 8

    def place(a):
        return jnp.clip(a - LEVELS[0], 0, len(LEVELS) - 1)

    def own_copy(k):
        return pltpu.make_async_copy(
            mine.at[k], land.at[pl.ds(k * per + comp * own, own)], mine_sem.at[k]
        )

    def combine(k):
        for copy in forward(k):
            copy.wait_recv()
        got[k, comp] = sent[pl.ds(k * per + comp * own, own)]
        for n, a in enumerate(LEVELS):
            total = jnp.zeros((own, 8, FLAT), jnp.float32)
            for g in range(GRIDS):
                weight = jnp.where(level_ref[g] == a, coef_ref[g], 0).astype(jnp.float32)
                total += weight * got[k, g]
            total = total.reshape(flat_rows, FLAT)
            res[n] = total
            high, low = split(total)
            lvl[n, pl.ds(0, flat_rows)] = high
            lvl[n, pl.ds(flat_rows, flat_rows)] = low
        for n, a in enumerate(LEVELS):
            value = jnp.zeros((2 * flat_rows, FLAT), jnp.float32)
            for m, other in enumerate([o for o in range(len(LEVELS)) if o != n]):
                value += dot(lvl[other], tab[n, pl.ds(m * FLAT, FLAT)])
            res[n] += value[:flat_rows] + value[flat_rows:]
        for g in range(GRIDS):
            back[k, g] = res[place(level_ref[g])].reshape(own, 8, FLAT)
        mine[k] = res[place(level)].reshape(own, 8, FLAT)
        own_copy(k).start()
        for copy in backward(k):
            copy.start()

    def stencil_outer(k):
        def halo(t, carry):
            m = k * (per // 2) + t
            up, dn = up8[m], dn8[m]
            u0[2 * m, pl.ds(cy, 8)] = jnp.where(lane_low, up, dn)
            u0[2 * m + 1, pl.ds(cy, 8)] = pltpu.roll(jnp.where(lane_low, dn, up), 4, 0)
            return carry

        lax.fori_loop(0, per // 2 + 4, halo, 0)
        early(k * per, per, cy + 8)
        late(per, cy + 8, "outer", (2 + k) * per)

    def start(copies):
        for copy in copies:
            copy.start()

    early(quarter, per, cy)
    pl.semaphore_wait(barrier, len(near) + len(PEERS))
    start(rims + sides[0] + corners + sides[1])
    late(per, cy, "inner", 0)
    start(forward(0))
    for copy in rims:
        copy.wait_recv()
    for n, first in enumerate((3 * quarter, 0)):
        early(first, quarter, cy)
        late(quarter, cy, "inner", per + n * quarter)
    start(forward(1))
    tab_copy.wait()
    for copy in sides[0] + corners:
        copy.wait_recv()
    combine(0)
    stencil_outer(0)
    start(forward(2))
    combine(1)
    for copy in sides[1]:
        copy.wait_recv()
    stencil_outer(1)
    start(forward(3))
    combine(2)
    combine(3)
    for copy in rims + corners + sides[0] + sides[1]:
        copy.wait_send()
    for k in range(4):
        for copy in forward(k):
            copy.wait_send()
        for copy in backward(k):
            copy.wait()
        own_copy(k).wait()


def finish(outer, inner, out):
    lane_low = lax.broadcasted_iota(jnp.int32, (8, FLAT), 0) < 4
    for x in range(outer.shape[0]):
        turned = pltpu.roll(inner[x], 4, 0)
        out[x, pl.ds(0, 8)] = jnp.where(lane_low, outer[x], turned)
        out[x, pl.ds(8, 8)] = jnp.where(lane_low, turned, outer[x])


def solution(mesh):
    table = exchange_table()

    def local(field, third_level, coefficients, rates, reaction):
        _, rows, cy, flat = field.shape
        per = rows // 2
        own = per // GRIDS
        tall = cy + 8
        height = per + 32
        hbm = pl.BlockSpec(memory_space=pltpu.HBM)
        f32, bf16 = jnp.float32, jnp.bfloat16
        dma = pltpu.SemaphoreType.DMA
        peers = len(PEERS)
        halos = 10
        landed = pl.pallas_call(
            kernel,
            out_shape=jax.ShapeDtypeStruct((2 * rows, 8, flat), f32),
            in_specs=[hbm] * 6,
            out_specs=hbm,
            scratch_shapes=[
                pltpu.SMEM(third_level.shape, jnp.int32),
                pltpu.SMEM(coefficients.shape, jnp.int32),
                pltpu.SMEM(rates.shape, f32),
                pltpu.SMEM(reaction.shape, f32),
                dma((4,)),
                pltpu.VMEM((rows + 24, tall, flat), f32),
                pltpu.VMEM((rows // 2 + 4, 8, flat), f32),
                pltpu.VMEM((rows // 2 + 4, 8, flat), f32),
                pltpu.VMEM((rows // 2 + 4, 8, flat), f32),
                pltpu.VMEM((rows // 2 + 4, 8, flat), f32),
                pltpu.VMEM((height, tall, flat), f32),
                pltpu.VMEM((height, tall, flat), f32),
                pltpu.VMEM((32 * tall, flat), f32),
                pltpu.VMEM((flat, flat), bf16),
                pltpu.VMEM((flat, flat), bf16),
                pltpu.VMEM((2 * rows, 8, flat), f32),
                pltpu.VMEM((4, GRIDS, own, 8, flat), f32),
                pltpu.VMEM((len(LEVELS), 2 * own * 8, flat), bf16),
                pltpu.VMEM((len(LEVELS), own * 8, flat), f32),
                pltpu.VMEM((4, GRIDS, own, 8, flat), f32),
                pltpu.VMEM((4, own, 8, flat), f32),
                dma((4,)),
                pltpu.VMEM(table.shape, bf16),
                dma((4,)),
                dma,
                dma((halos,)),
                dma((halos,)),
                dma((4, peers)),
                dma((4, peers)),
                dma((4, peers)),
                dma((4, peers)),
            ],
            compiler_params=pltpu.CompilerParams(
                collective_id=0, has_side_effects=True, vmem_limit_bytes=64900000
            ),
        )(field[0], jnp.asarray(table), third_level, coefficients, rates, reaction)
        step = rows // 4
        result = pl.pallas_call(
            finish,
            out_shape=jax.ShapeDtypeStruct((rows, cy, flat), f32),
            grid=(4,),
            in_specs=[
                pl.BlockSpec((step, 8, flat), lambda i: (4 + i, 0, 0)),
                pl.BlockSpec((step, 8, flat), lambda i: ((i + 3) % 4, 0, 0)),
            ],
            out_specs=pl.BlockSpec((step, cy, flat), lambda i: (i, 0, 0)),
        )(landed, landed)
        return result[None]

    return jax.shard_map(
        local,
        mesh=mesh,
        in_specs=(P("comp", "gx", "gy", None), P(), P(), P(), P()),
        out_specs=P("comp", "gx", "gy", None),
        check_vma=False,
    )
```

time: 76.7 us -> 72.9 us (0.950)
  local copies, waits for them, and re-layouts: 3.08 us -> 0 us
  Pallas kernels: 72.9 us -> 72.1 us
    unnamed x1 -> x0, local copies, waits for them, and re-layouts: 3.08 us -> none
    pallas_call x1 -> x2, Pallas kernels: 72.9 us -> 72.1 us  [the longest x1 68.3 us: local(): pl.pallas_call(kernel, out_shape=jax.ShapeDtypeStruct((2 * rows, 8, flat)...]
where the time goes in v2:
time: 72.9 us; the launch traced here: 72.8 us
  Pallas kernels  72.1 us (99%)
    pallas_call x1, Pallas kernels, local(): pl.pallas_call(kernel, out_shape=jax.ShapeDtypeStruct((2 * rows, 8, flat)...  68.3 us
    pallas_call x1, Pallas kernels, local(): pl.pallas_call(finish, out_shape=jax.ShapeDtypeStruct((rows, cy, flat), f...  3.77 us

profile of v2, /device:TPU:1, one launch (start us, length us, event | category | flops | bytes accessed | tf_op | source)
XLA Modules:
  0.0 72.8 jit_solution(17372887112235656131)
XLA Ops:
  0.7 68.3 %shard_map.64.outer.inner = f32[256,8,256]{2,1,0:T(8,128)} custom-call(f32[128,16,256]{2,1,0:T(8,128)} %bitcast.2, bf16[5,1024,256]{2,1,0:T(8,128)(2,1)} %constant.2.clone.table, s32[16]{0:T(128)} %level_in.1, s32[16]{0:T(128)} %coef_in.1, f32[2,4]{1,0:T(2,128)} %rate_in.1, f32[1]{0:T(128)S(6)} %copy.7.react_in), custom_call_target="tpu_custom_call" | custom-call | tf_op jit(solution)/shard_map/pallas_call | solution.py:372
  69.0 3.8 %shard_map.65 = f32[128,16,256]{2,1,0:T(8,128)} custom-call(f32[256,8,256]{2,1,0:T(8,128)} %shard_map.64.outer.inner, f32[256,8,256]{2,1,0:T(8,128)} %shard_map.64.outer.inner), custom_call_target="tpu_custom_call" | custom-call | tf_op jit(solution)/shard_map/pallas_call | solution.py:415

commit v3 on v2

--- a/solution.py
+++ b/solution.py
@@ -15,7 +15,7 @@
 LEVELS = (2, 3, 4, 5, 6)
 FLAT = 256
 GRIDS = 16
-BLOCK = 16
+BLOCK = 32
 ORDER = [(1, 0), (0, 1), (3, 0), (1, 1), (2, 0), (3, 1), (2, 1)]
 PEERS = [(y, z, c) for y, z in ORDER for c in (0, 1)] + [(0, 0, 1)]
 
@@ -347,12 +347,39 @@
         own_copy(k).wait()
 
 
-def finish(outer, inner, out):
+def finish(landed, result, held, done, in_sem, out_sem):
+    rows = result.shape[0]
+    step = rows // 4
     lane_low = lax.broadcasted_iota(jnp.int32, (8, FLAT), 0) < 4
-    for x in range(outer.shape[0]):
-        turned = pltpu.roll(inner[x], 4, 0)
-        out[x, pl.ds(0, 8)] = jnp.where(lane_low, outer[x], turned)
-        out[x, pl.ds(8, 8)] = jnp.where(lane_low, turned, outer[x])
+
+    def bring(i):
+        part = pl.ds(i * step, step)
+        return pltpu.make_async_copy(landed.at[part], held.at[part], in_sem.at[i])
+
+    def put(i):
+        part = pl.ds(i * step, step)
+        return pltpu.make_async_copy(done.at[part], result.at[part], out_sem.at[i])
+
+    for i in range(4):
+        bring(4 + i).start()
+        bring((i + 3) % 4).start()
+    for i in range(4):
+        bring(4 + i).wait()
+        bring((i + 3) % 4).wait()
+
+        def rows_of(t, carry):
+            for n in range(4):
+                x = t * 4 + n
+                outer = held[rows + i * step + x]
+                turned = pltpu.roll(held[(i + 3) % 4 * step + x], 4, 0)
+                done[i * step + x, pl.ds(0, 8)] = jnp.where(lane_low, outer, turned)
+                done[i * step + x, pl.ds(8, 8)] = jnp.where(lane_low, turned, outer)
+            return carry
+
+        lax.fori_loop(0, step // 4, rows_of, 0)
+        put(i).start()
+    for i in range(4):
+        put(i).wait()
 
 
 def solution(mesh):
@@ -411,17 +438,19 @@
                 collective_id=0, has_side_effects=True, vmem_limit_bytes=64900000
             ),
         )(field[0], jnp.asarray(table), third_level, coefficients, rates, reaction)
-        step = rows // 4
         result = pl.pallas_call(
             finish,
             out_shape=jax.ShapeDtypeStruct((rows, cy, flat), f32),
-            grid=(4,),
-            in_specs=[
-                pl.BlockSpec((step, 8, flat), lambda i: (4 + i, 0, 0)),
-                pl.BlockSpec((step, 8, flat), lambda i: ((i + 3) % 4, 0, 0)),
+            in_specs=[hbm],
+            out_specs=hbm,
+            scratch_shapes=[
+                pltpu.VMEM((2 * rows, 8, flat), f32),
+                pltpu.VMEM((rows, cy, flat), f32),
+                dma((8,)),
+                dma((4,)),
             ],
-            out_specs=pl.BlockSpec((step, cy, flat), lambda i: (i, 0, 0)),
-        )(landed, landed)
+            compiler_params=pltpu.CompilerParams(vmem_limit_bytes=64900000),
+        )(landed)
         return result[None]
 
     return jax.shard_map(

time: 72.9 us -> 71.6 us (0.982)
  Pallas kernels: 72.1 us -> 70.8 us
    pallas_call x1, Pallas kernels: 3.77 us -> 2.5 us  [local(): pl.pallas_call(finish, out_shape=jax.ShapeDtypeStruct((rows, cy, flat), f...]
where the time goes in v3:
time: 71.6 us; the launch traced here: 71.4 us
  Pallas kernels  70.8 us (99%)
    pallas_call x1, Pallas kernels, local(): pl.pallas_call(kernel, out_shape=jax.ShapeDtypeStruct((2 * rows, 8, flat)...  68.3 us
    pallas_call x1, Pallas kernels, local(): pl.pallas_call(finish, out_shape=jax.ShapeDtypeStruct((rows, cy, flat), f...  2.5 us

profile of v3, /device:TPU:1, one launch (start us, length us, event | category | flops | bytes accessed | tf_op | source)
XLA Modules:
  0.0 71.4 jit_solution(3452066533178680203)
XLA Ops:
  0.7 68.3 %shard_map.64.landed = f32[256,8,256]{2,1,0:T(8,128)} custom-call(f32[128,16,256]{2,1,0:T(8,128)} %bitcast.2, bf16[5,1024,256]{2,1,0:T(8,128)(2,1)} %constant.2.clone.table, s32[16]{0:T(128)} %level_in.1, s32[16]{0:T(128)} %coef_in.1, f32[2,4]{1,0:T(2,128)} %rate_in.1, f32[1]{0:T(128)S(6)} %copy.7.react_in), custom_call_target="tpu_custom_call" | custom-call | tf_op jit(solution)/shard_map/pallas_call | solution.py:399
  68.9 2.5 %shard_map.65 = f32[128,16,256]{2,1,0:T(8,128)} custom-call(f32[256,8,256]{2,1,0:T(8,128)} %shard_map.64.landed), custom_call_target="tpu_custom_call" | custom-call | tf_op jit(solution)/shard_map/pallas_call | solution.py:441
